TPU v7x, 256 devices: a whole 4x4x8 slice. The times are simulated.
256 devices in a mesh: batch: 128 (over x_hi, y, z, core), rep: 2 (over x_lo).
Axes of the slice: x: 4 (x_hi: 2, x_lo: 2; x = x_hi * 2 + x_lo), y: 4, z: 8, core: 2. Of those that a mesh axis runs over, the one named last changes fastest.
Arguments:
- image_embed: bfloat16 [16384, 1024], P('batch'), may hold values from -2 to 2
- text_embed: bfloat16 [16384, 1024], P(('batch', 'rep')), may hold values from -2 to 2
- logit_scale: float32 [1], replicated, may hold values from 50 to 100
Outputs:
- mean_loss: float32 [], replicated
- image_grad: float32 [16384, 1024], P(('batch', 'rep'))
- text_grad: float32 [16384, 1024], P(('batch', 'rep'))
All inputs are finite; a program needn't handle non-finite values.
Results may differ from a plain program's by a relative error of at most 0.0025.
Values may be sent and summed in bfloat16 or wider, within the bound.
No kernel may reach another device: no remote copies, remote signals or barrier semaphores. Data moves between devices by JAX's collectives and lax.ppermute only.
A program may use at most 128 MiB of HBM per device.

v0:
```python
import functools
import jax
import jax.numpy as jnp
from jax import lax
from jax.sharding import Mesh
from jax.sharding import PartitionSpec as P

BATCH = ("batch_0", "batch_1", "batch_2", "batch_3")
BATCH_REP = ("batch_0", "batch_1", "batch_2", "batch_3", "rep")


def copy_for_each(array, axis):
    peers = lax.axis_size(axis)
    return lax.all_to_all(
        jnp.broadcast_to(array[None], (peers, *array.shape)), axis, 0, 0, tiled=True
    )


def all_in_one(array, axis):
    leaves = jax.tree.leaves(array)
    sequence = sorted(range(len(leaves)), key=lambda k: -leaves[k].size)
    width = (1, *leaves[sequence[0]].shape)[-1]
    lines = [
        jnp.pad(leaves[k].reshape(-1), (0, -leaves[k].size % width)).reshape(-1, width)
        for k in sequence
    ]
    both, at, found = (copy_for_each(jnp.concatenate(lines), axis), 0, {})
    for k, line in zip(sequence, lines):
        share = both[:, at : at + len(line)].reshape(len(both), -1)
        found[k] = share[:, : leaves[k].size].reshape(-1, *leaves[k].shape)
        at += len(line)
    numbers = iter(range(len(leaves)))
    return jax.tree.map(lambda _: found[next(numbers)], array)


def joined_by_halves(pieces, combine):
    while len(jax.tree.leaves(pieces)[0]) > 1:
        pieces = jax.vmap(combine)(
            *(jax.tree.map(lambda part: part[side::2], pieces) for side in (0, 1))
        )
    return jax.tree.map(lambda part: part[0], pieces)


def merged(array, axis, combine):
    pieces = all_in_one(array, axis)
    return joined_by_halves(pieces, combine)


def collected_together(array, axis):
    leaves = jax.tree.leaves(array)
    sequence = sorted(range(len(leaves)), key=lambda k: -leaves[k].size)
    width = (1, *leaves[sequence[0]].shape)[-1]
    lines = [
        jnp.pad(leaves[k].reshape(-1), (0, -leaves[k].size % width)).reshape(-1, width)
        for k in sequence
    ]
    both, at, found = (lax.all_gather(jnp.concatenate(lines), axis), 0, {})
    for k, line in zip(sequence, lines):
        share = both[:, at : at + len(line)].reshape(len(both), -1)
        found[k] = share[:, : leaves[k].size].reshape(-1, *leaves[k].shape)
        at += len(line)
    numbers = iter(range(len(leaves)))
    return jax.tree.map(lambda _: found[next(numbers)], array)


def merged_by_axis(array, axes, combine):
    for axis in axes:
        pieces = collected_together(array, axis)
        array = jax.tree.map(lambda part: part[0], pieces)
        for k in range(1, lax.axis_size(axis)):
            array = combine(array, jax.tree.map(lambda part: part[k], pieces))
    return array


def over_axes(array, axes):
    return functools.reduce(lax.psum, axes, array)


def cut_along(array, dim, peers):
    lengths = array.shape
    parts = array.reshape(*lengths[:dim], peers, lengths[dim] // peers, *lengths[dim + 1 :])
    return jnp.moveaxis(parts, dim, 0)


def sum_at_owner(array, axis, dim):
    parts = cut_along(array, dim, lax.axis_size(axis))
    arrived = lax.all_to_all(parts, axis, split_axis=0, concat_axis=0, tiled=True)
    return arrived.sum(axis=0)


def combine_lse(earlier, later):
    biggest = jnp.maximum(earlier[0], later[0])
    return (
        biggest,
        earlier[1] * jnp.exp(earlier[0] - biggest) + later[1] * jnp.exp(later[0] - biggest),
    )


def body(image_embed, text_embed, logit_scale):
    scale_value = logit_scale[0]
    row_count = image_embed.shape[0]
    half_rows = text_embed.shape[0]
    batch_count = lax.axis_size(BATCH)
    batch_index = lax.axis_index(BATCH)
    rep_index = lax.axis_index("rep")
    whole_text = lax.all_gather(text_embed, BATCH, axis=0, tiled=True)
    scores = scale_value * lax.dot_general(
        image_embed, whole_text, (((1,), (1,)), ((), ())), preferred_element_type=jnp.float32
    )
    row_max = jnp.max(scores, axis=1)
    row_sum = jnp.sum(jnp.exp(scores - row_max[:, None]), axis=1)
    row_max, row_sum = merged((row_max, row_sum), "rep", combine_lse)
    row_lse = row_max + jnp.log(row_sum)
    column_max = jnp.max(scores, axis=0)
    column_sum = jnp.sum(jnp.exp(scores - column_max[None, :]), axis=0)
    column_max, column_sum = merged_by_axis((column_max, column_sum), BATCH, combine_lse)
    col_lse = column_max + jnp.log(column_sum)
    own_lse = lax.dynamic_slice_in_dim(col_lse, batch_index * half_rows, half_rows, 0)
    own_scores = lax.dynamic_slice(
        scores, (rep_index * half_rows, batch_index * half_rows), (half_rows, half_rows)
    )
    own_diag = jnp.diagonal(own_scores)
    own_rows = lax.dynamic_slice_in_dim(row_lse, rep_index * half_rows, half_rows, 0)
    loss_sum = over_axes(jnp.sum(own_rows + own_lse - 2.0 * own_diag), BATCH_REP)
    mean_loss = loss_sum / (2 * row_count * batch_count)
    row_ids = lax.broadcasted_iota(jnp.int32, scores.shape, 0) - rep_index * half_rows
    column_ids = lax.broadcasted_iota(jnp.int32, scores.shape, 1) - batch_index * half_rows
    diag_match = ((row_ids == column_ids) & (column_ids >= 0) & (column_ids < half_rows)).astype(
        jnp.float32
    )
    weights = (
        jnp.exp(scores - row_lse[:, None]) + jnp.exp(scores - col_lse[None, :]) - 2.0 * diag_match
    ).astype(jnp.bfloat16)
    image_part = (
        scale_value * 0.5 * jnp.dot(weights, whole_text, preferred_element_type=jnp.float32)
    )
    image_grad = sum_at_owner(image_part, "rep", 0)
    all_rows_lse = lax.all_gather(row_lse, BATCH, axis=0, tiled=True)
    own_first = (2 * batch_index + rep_index) * half_rows
    fragment = lax.all_gather(image_embed, BATCH, axis=0, tiled=True)
    scores_back = scale_value * lax.dot_general(
        text_embed, fragment, (((1,), (1,)), ((), ())), preferred_element_type=jnp.float32
    )
    image_ids = lax.broadcasted_iota(jnp.int32, scores_back.shape, 1)
    text_ids = own_first + lax.broadcasted_iota(jnp.int32, scores_back.shape, 0)
    back_match = (image_ids == text_ids).astype(jnp.float32)
    weights_block = (
        jnp.exp(scores_back - own_lse[:, None])
        + jnp.exp(scores_back - all_rows_lse[None, :])
        - 2.0 * back_match
    ).astype(jnp.bfloat16)
    summed = jnp.dot(weights_block, fragment, preferred_element_type=jnp.float32)
    text_grad = scale_value * 0.5 * summed
    return (mean_loss, image_grad, text_grad)


def solution(mesh):
    split = Mesh(
        mesh.devices.reshape(2, 4, 8, 2, mesh.shape["rep"]),
        ("batch_0", "batch_1", "batch_2", "batch_3", "rep"),
    )
    placed = (P(BATCH, None), P(BATCH_REP, None), P())
    return jax.shard_map(
        body,
        mesh=split,
        in_specs=placed,
        out_specs=(P(), P(BATCH_REP, None), P(BATCH_REP, None)),
        check_vma=False,
    )
```

profile of v0, /device:TPU:1, one launch (start us, length us, event | category | flops | bytes accessed | tf_op | source)
XLA Modules:
  0.0 527.8 jit_solution(11438516798877127760)
XLA Ops:
  7.2 0.0 all-gather.12.cloned.1.call-start
  7.2 0.7 all-gather.12.cloned.1.call-update
  7.9 0.0 all-gather.14.cloned.1.call-start
  7.9 0.7 all-gather.14.cloned.1.call-update
  9.4 157.7 %all-gather.12.cloned.1.call-done = bf16[8192,1024]{1,0:T(8,128)(2,1)} async-done(((bf16[64,1024]{1,0:T(8,128)(2,1)}), bf16[8192,1024]{1,0:T(8,128)(2,1)}) %all-gather.12.cloned.1.call-update) | async-done | bytes 16777232 | tf_op jit(solution)/shard_map/all_gather | solution.py:106
  167.1 13.5 %fusion.72 = (f32[128]{0:T(128)S(1)}, f32[8192]{0:T(1024)S(1)}, f32[128,8192]{1,0:T(8,128)}) fusion(bf16[128,1024]{1,0:T(8,128)(2,1)} %param.3, bf16[8192,1024]{1,0:T(8,128)(2,1)} %all-gather.12.cloned.1.call-done, f32[]{:T(128)} %bitcast.315), kind=kOutput, calls=%fused_computation.126 | convolution fusion | flops 2150621184 | bytes 21266948 | tf_op jit(solution)/shard_map/dot_general | solution.py:107
  180.7 3.6 exponential_reduce_fusion.1
  184.2 0.6 broadcast_in_dim.4
  184.8 3.2 all-to-all-start
  188.1 0.1 maximum_bitcast_fusion
  188.1 5.3 %all-gather.4 = f32[2,2,8192]{2,1,0:T(2,128)S(1)} all-gather(f32[1,2,8192]{2,1,0:T(2,128)S(1)} %maximum_bitcast_fusion), channel_id=2, replica_groups=mesh['batch_0'=2,'batch_1'=4,'batch_2'=8,'batch_3'=2,'rep'=2] {'batch_0'}, dimensions={0}, use_global_device_ids=true | all-gather | bytes 196608 | tf_op jit(solution)/shard_map/all_gather | solution.py:57
  193.4 0.1 fusion.47
  193.5 0.1 maximum_bitcast_fusion.1
  193.6 11.0 %all-gather.5 = f32[4,2,8192]{2,1,0:T(2,128)S(1)} all-gather(f32[1,2,8192]{2,1,0:T(2,128)S(1)} %maximum_bitcast_fusion.1), channel_id=3, replica_groups=mesh['batch_0'=2,'batch_1'=4,'batch_2'=8,'batch_3'=2,'rep'=2] {'batch_1'}, dimensions={0}, use_global_device_ids=true | all-gather | bytes 327680 | tf_op jit(solution)/shard_map/all_gather | solution.py:57
  204.6 0.3 fusion.38
  204.9 0.1 maximum_bitcast_fusion.2
  205.0 21.2 %all-gather.6 = f32[8,2,8192]{2,1,0:T(2,128)S(1)} all-gather(f32[1,2,8192]{2,1,0:T(2,128)S(1)} %maximum_bitcast_fusion.2), channel_id=4, replica_groups=mesh['batch_0'=2,'batch_1'=4,'batch_2'=8,'batch_3'=2,'rep'=2] {'batch_2'}, dimensions={0}, use_global_device_ids=true | all-gather | bytes 589824 | tf_op jit(solution)/shard_map/all_gather | solution.py:57
  226.2 0.7 fusion.17
  226.9 0.1 maximum_bitcast_fusion.3
  227.0 9.8 %all-gather.7 = f32[2,2,8192]{2,1,0:T(2,128)S(1)} all-gather(f32[1,2,8192]{2,1,0:T(2,128)S(1)} %maximum_bitcast_fusion.3), channel_id=5, replica_groups=mesh['batch_0'=2,'batch_1'=4,'batch_2'=8,'batch_3'=2,'rep'=2] {'batch_3'}, dimensions={0}, use_global_device_ids=true | all-gather | bytes 196608 | tf_op jit(solution)/shard_map/all_gather | solution.py:57
  236.8 0.1 fusion.76
  236.9 0.8 dynamic_slice.11
  237.8 0.8 gather_fusion
  238.6 0.0 all-to-all-done
  238.6 0.7 subtract_reduce_fusion
  239.3 5.9 %psum.35 = f32[]{:T(128)} all-reduce(f32[]{:T(128)} %get-tuple-element.7), channel_id=1, replica_groups=mesh['batch_0'=2,'batch_1'=4,'batch_2'=8,'batch_3'=2,'rep'=2] {'batch_0'}, use_global_device_ids=true, to_apply=%region_5.6 | all-reduce | flops 1 | bytes 8 | tf_op jit(solution)/shard_map/psum | solution.py:76
  245.2 9.5 %psum.36 = f32[]{:T(128)} all-reduce(f32[]{:T(128)} %psum.35), channel_id=1, replica_groups=mesh['batch_0'=2,'batch_1'=4,'batch_2'=8,'batch_3'=2,'rep'=2] {'batch_1'}, use_global_device_ids=true, to_apply=%region_6.7 | all-reduce | flops 1 | bytes 8 | tf_op jit(solution)/shard_map/psum | solution.py:76
  254.7 13.1 %psum.37 = f32[]{:T(128)} all-reduce(f32[]{:T(128)} %psum.36), channel_id=1, replica_groups=mesh['batch_0'=2,'batch_1'=4,'batch_2'=8,'batch_3'=2,'rep'=2] {'batch_2'}, use_global_device_ids=true, to_apply=%region_7.8 | all-reduce | flops 1 | bytes 8 | tf_op jit(solution)/shard_map/psum | solution.py:76
  267.8 9.0 %psum.38 = f32[]{:T(128)} all-reduce(f32[]{:T(128)} %psum.37), channel_id=1, replica_groups=mesh['batch_0'=2,'batch_1'=4,'batch_2'=8,'batch_3'=2,'rep'=2] {'batch_3'}, use_global_device_ids=true, to_apply=%region_8.9 | all-reduce | flops 1 | bytes 8 | tf_op jit(solution)/shard_map/psum | solution.py:76
  276.9 0.0 copy-start
  276.9 11.5 %fusion.14 = f32[128,1024]{1,0:T(8,128)} fusion(bf16[8192,1024]{1,0:T(8,128)(2,1)} %all-gather.12.cloned.1.call-done, f32[128,8192]{1,0:T(8,128)} %get-tuple-element.19, s32[8192]{0:T(1024)S(1)} %iota_subtract_fusion, f32[8192]{0:T(1024)S(1)} %log_add_fusion, f32[128]{0:T(128)S(1)} %log_add_fusion.1, s32[128]{0:T(128)S(1)} %iota_subtract_fusion.1, ...), kind=kOutput, calls=%fused_computation.22 | convolution fusion | flops 2157051904 | bytes 21578756 | tf_op jit(solution)/shard_map/dot_general | solution.py:135
  288.4 3.5 all-to-all-start.1
  291.9 15.4 %psum.39 = f32[]{:T(128)} all-reduce(f32[]{:T(128)} %psum.38), channel_id=1, replica_groups=mesh['batch_0'=2,'batch_1'=4,'batch_2'=8,'batch_3'=2,'rep'=2] {'rep'}, use_global_device_ids=true, to_apply=%region_9.10 | all-reduce | flops 1 | bytes 8 | tf_op jit(solution)/shard_map/psum | solution.py:76
  308.0 179.3 %all-gather.8 = f32[128,1,128]{2,1,0:T(1,128)S(1)} all-gather(f32[1,1,128]{2,1,0:T(1,128)S(1)} %fusion.83), channel_id=1, replica_groups=mesh['batch_0'=2,'batch_1'=4,'batch_2'=8,'batch_3'=2,'rep'=2] {'batch_0'..., dimensions={0}, use_global_device_ids=true | all-gather | bytes 66048 | tf_op jit(solution)/shard_map/all_gather | solution.py:138
  487.2 0.0 all-to-all-done.1
  487.2 0.7 reduce_sum.39
  488.0 0.0 all-gather.14.cloned.1.call-done
  488.0 0.0 copy-done
  488.0 31.9 %fusion.15 = f32[64,1024]{1,0:T(8,128)} fusion(bf16[16384,1024]{1,0:T(8,128)(2,1)} %all-gather.14.cloned.1.call-done, bf16[64,1024]{1,0:T(8,128)(2,1)S(1)} %copy-done, s32[64]{0:T(128)S(1)} %iota_add_fusion, f32[16384]{0:T(1024)S(1)} %bitcast.318, f32[64]{0:T(128)S(1)} %get-tuple-element.8, f32[]{:T(128)} %bitcast.317, f32[]{:T(128)S(6)} %mul.358), kind=kOutput, calls=%fused_computation.23 | convolution fusion | flops 4303421440 | bytes 34013704 | tf_op jit(solution)/shard_map/dot_general | solution.py:152
  (9 shorter events, 0.1 us)
Async XLA Ops:
  7.2 159.9 %all-gather.12.cloned.1.call-start = ((), (), s32[]{:S(2)}) async-start(), calls=%async_computation.2 | async-start | bytes 16908288 | tf_op jit(solution)/shard_map/all_gather | solution.py:106
  7.9 480.1 %all-gather.14.cloned.1.call-start = ((), (), s32[]{:S(2)}) async-start(), calls=%async_computation.3 | async-start | bytes 33816576 | tf_op jit(solution)/shard_map/all_gather | solution.py:140
  184.8 53.7 %all-to-all-start = ((f32[2,2,128]{2,1,0:T(2,128)}), f32[2,2,128]{2,1,0:T(2,128)S(1)}, u32[]{:S(2)}, u32[]{:S(2)}) async-start(f32[2,2,128]{2,1,0:T(2,128)} %broadcast_in_dim.4), calls=%async_computation | async-start | bytes 4096 | tf_op jit(solution)/shard_map/all_to_all | solution.py:14
  276.9 211.1 %copy-start = (bf16[64,1024]{1,0:T(8,128)(2,1)S(1)}, bf16[64,1024]{1,0:T(8,128)(2,1)}, u32[]{:S(2)}) copy-start(bf16[64,1024]{1,0:T(8,128)(2,1)} %param.4) | copy-start | bytes 393220
  288.4 198.9 %all-to-all-start.1 = ((f32[2,64,1024]{2,1,0:T(8,128)}), f32[2,64,1024]{2,1,0:T(8,128)S(1)}, u32[]{:S(2)}, u32[]{:S(2)}) async-start(f32[2,64,1024]{2,1,0:T(8,128)} %bitcast.46), calls=%async_computation.1 | async-start | bytes 1048576 | tf_op jit(solution)/shard_map/all_to_all | solution.py:87
Sparse Core Ops, SparseCore 0:
  11.6 155.4 all-gather.11
  170.7 214.5 all-gather.13
where the time goes:
time: 528 us
  blocking collectives  280 us (53%)
  waiting for transfers between devices  159 us (30%)
  matrix products  56.9 us (11%)
  between operations  16.6 us (3%)
  starting transfers between devices  6.79 us (1%)
  other arithmetic  6.55 us (1%)
    all_gather x1, blocking collectives, body(): all_rows_lse = lax.all_gather(row_lse, BATCH, axis=0, tiled=True)  179 us
    all_gather x1, waiting for transfers between devices, body(): whole_text = lax.all_gather(text_embed, BATCH, axis=0, tiled=True)  158 us
    psum x5, blocking collectives, over_axes(): return functools.reduce(lax.psum, axes, array)  53 us
    all_gather x4, blocking collectives, collected_together(): both, at, found = (lax.all_gather(jnp.concatenate(lines), axis), 0, {})  47.2 us
    dot_general x1, matrix products, body(): jnp.dot(weights_block, fragment, preferred_element_type=jnp.float32)  31.9 us
    dot_general x1, matrix products, body(): lax.dot_general(image_embed, whole_text, (((1,), (1,)), ((), ())), prefer...  13.5 us
    dot_general x1, matrix products, body(): jnp.dot(weights, whole_text, preferred_element_type=jnp.float32)  11.5 us
  transfers between devices with their start and end apart: 4, of which 1 were waited for; matrix products, arithmetic and copies ran while one was open for 6% of the time, Pallas kernels for 0%

commit v1 on v0

--- a/solution.py
+++ b/solution.py
@@ -135,7 +135,12 @@
         scale_value * 0.5 * jnp.dot(weights, whole_text, preferred_element_type=jnp.float32)
     )
     image_grad = sum_at_owner(image_part, "rep", 0)
-    all_rows_lse = lax.all_gather(row_lse, BATCH, axis=0, tiled=True)
+    all_rows_lse = jnp.concatenate(
+        lax.all_to_all(
+            jnp.stack(lax.axis_size(BATCH) * [row_lse]), BATCH, split_axis=0, concat_axis=0
+        ),
+        0,
+    )
     own_first = (2 * batch_index + rep_index) * half_rows
     fragment = lax.all_gather(image_embed, BATCH, axis=0, tiled=True)
     scores_back = scale_value * lax.dot_general(

time: 528 us -> 421 us (0.80)
  blocking collectives: 280 us -> 91.9 us
  waiting for transfers between devices: 159 us -> 229 us
  starting transfers between devices: 6.79 us -> 15.8 us
    all_gather x1 -> x0, blocking collectives: 179 us -> none  [body(): all_rows_lse = lax.all_gather(row_lse, BATCH, axis=0, tiled=True)]
    all_gather x1, waiting for transfers between devices: 0.01 us -> 63.3 us  [body(): fragment = lax.all_gather(image_embed, BATCH, axis=0, tiled=True)]
    all_to_all x0 -> x1, starting transfers between devices: none -> 8.87 us  [body(): lax.all_to_all(jnp.stack(lax.axis_size(BATCH) * [row_lse]), BATCH, split_...]
    psum x5, blocking collectives: 53 us -> 44.7 us  [over_axes(): return functools.reduce(lax.psum, axes, array)]
    all_to_all x1, waiting for transfers between devices: 0.01 us -> 6.68 us  [sum_at_owner(): lax.all_to_all(parts, axis, split_axis=0, concat_axis=0, tiled=True)]
  transfers between devices with their start and end apart: 4 -> 5, of which waited for: 1 -> 3; matrix products, arithmetic and copies ran while one was open for 6% -> 8% of each run, Pallas kernels for 0% -> 0%
where the time goes in v1:
time: 421 us; the launch traced here: 420 us
  waiting for transfers between devices  229 us (54%)
  blocking collectives  91.9 us (22%)
  matrix products  57.2 us (14%)
  between operations  16.6 us (4%)
  starting transfers between devices  15.8 us (4%)
  other arithmetic  6.53 us (2%)
    all_gather x1, waiting for transfers between devices, body(): whole_text = lax.all_gather(text_embed, BATCH, axis=0, tiled=True)  158 us
    all_gather x1, waiting for transfers between devices, body(): fragment = lax.all_gather(image_embed, BATCH, axis=0, tiled=True)  63.3 us
    all_gather x4, blocking collectives, collected_together(): both, at, found = (lax.all_gather(jnp.concatenate(lines), axis), 0, {})  47.2 us
    psum x5, blocking collectives, over_axes(): return functools.reduce(lax.psum, axes, array)  44.7 us
    dot_general x1, matrix products, body(): jnp.dot(weights_block, fragment, preferred_element_type=jnp.float32)  31.9 us
    dot_general x1, matrix products, body(): lax.dot_general(image_embed, whole_text, (((1,), (1,)), ((), ())), prefer...  13.5 us
    dot_general x1, matrix products, body(): jnp.dot(weights, whole_text, preferred_element_type=jnp.float32)  11.7 us
    all_to_all x1, starting transfers between devices, body(): lax.all_to_all(jnp.stack(lax.axis_size(BATCH) * [row_lse]), BATCH, split_...  8.87 us
  transfers between devices with their start and end apart: 5, of which 3 were waited for; matrix products, arithmetic and copies ran while one was open for 8% of the time, Pallas kernels for 0%

profile of v1, /device:TPU:1, one launch (start us, length us, event | category | flops | bytes accessed | tf_op | source)
XLA Modules:
  0.0 420.2 jit_solution(7607220219119610006)
XLA Ops:
  7.2 0.0 all-gather.11.cloned.1.call-start
  7.2 0.7 all-gather.11.cloned.1.call-update
  7.9 0.0 all-gather.13.cloned.1.call-start
  7.9 0.7 all-gather.13.cloned.1.call-update
  9.4 157.8 %all-gather.11.cloned.1.call-done = bf16[8192,1024]{1,0:T(8,128)(2,1)} async-done(((bf16[64,1024]{1,0:T(8,128)(2,1)}), bf16[8192,1024]{1,0:T(8,128)(2,1)}) %all-gather.11.cloned.1.call-update) | async-done | bytes 16777232 | tf_op jit(solution)/shard_map/all_gather | solution.py:106
  167.1 13.5 %fusion.72 = (f32[128]{0:T(128)S(1)}, f32[8192]{0:T(1024)S(1)}, f32[128,8192]{1,0:T(8,128)}) fusion(bf16[128,1024]{1,0:T(8,128)(2,1)} %param.3, bf16[8192,1024]{1,0:T(8,128)(2,1)} %all-gather.11.cloned.1.call-done, f32[]{:T(128)} %bitcast.305), kind=kOutput, calls=%fused_computation.126 | convolution fusion | flops 2150621184 | bytes 21266948 | tf_op jit(solution)/shard_map/dot_general | solution.py:107
  180.7 3.6 exponential_reduce_fusion.1
  184.2 0.6 broadcast_in_dim.4
  184.8 3.2 all-to-all-start
  188.1 0.1 maximum_bitcast_fusion
  188.1 5.3 %all-gather.4 = f32[2,2,8192]{2,1,0:T(2,128)S(1)} all-gather(f32[1,2,8192]{2,1,0:T(2,128)S(1)} %maximum_bitcast_fusion), channel_id=2, replica_groups=mesh['batch_0'=2,'batch_1'=4,'batch_2'=8,'batch_3'=2,'rep'=2] {'batch_0'}, dimensions={0}, use_global_device_ids=true | all-gather | bytes 196608 | tf_op jit(solution)/shard_map/all_gather | solution.py:57
  193.4 0.1 fusion.47
  193.5 0.1 maximum_bitcast_fusion.1
  193.6 11.0 %all-gather.5 = f32[4,2,8192]{2,1,0:T(2,128)S(1)} all-gather(f32[1,2,8192]{2,1,0:T(2,128)S(1)} %maximum_bitcast_fusion.1), channel_id=3, replica_groups=mesh['batch_0'=2,'batch_1'=4,'batch_2'=8,'batch_3'=2,'rep'=2] {'batch_1'}, dimensions={0}, use_global_device_ids=true | all-gather | bytes 327680 | tf_op jit(solution)/shard_map/all_gather | solution.py:57
  204.6 0.3 fusion.38
  204.9 0.1 maximum_bitcast_fusion.2
  205.0 21.2 %all-gather.6 = f32[8,2,8192]{2,1,0:T(2,128)S(1)} all-gather(f32[1,2,8192]{2,1,0:T(2,128)S(1)} %maximum_bitcast_fusion.2), channel_id=4, replica_groups=mesh['batch_0'=2,'batch_1'=4,'batch_2'=8,'batch_3'=2,'rep'=2] {'batch_2'}, dimensions={0}, use_global_device_ids=true | all-gather | bytes 589824 | tf_op jit(solution)/shard_map/all_gather | solution.py:57
  226.2 0.7 fusion.17
  226.9 0.1 maximum_bitcast_fusion.3
  227.0 9.8 %all-gather.7 = f32[2,2,8192]{2,1,0:T(2,128)S(1)} all-gather(f32[1,2,8192]{2,1,0:T(2,128)S(1)} %maximum_bitcast_fusion.3), channel_id=5, replica_groups=mesh['batch_0'=2,'batch_1'=4,'batch_2'=8,'batch_3'=2,'rep'=2] {'batch_3'}, dimensions={0}, use_global_device_ids=true | all-gather | bytes 196608 | tf_op jit(solution)/shard_map/all_gather | solution.py:57
  236.8 0.1 fusion.76
  236.9 0.0 all-to-all-done
  236.9 0.0 copy-start
  236.9 11.7 %fusion.14 = f32[128,1024]{1,0:T(8,128)} fusion(bf16[8192,1024]{1,0:T(8,128)(2,1)} %all-gather.11.cloned.1.call-done, f32[128,8192]{1,0:T(8,128)} %get-tuple-element.19, s32[8192]{0:T(1024)S(1)} %iota_subtract_fusion, f32[8192]{0:T(1024)S(1)} %log_add_fusion, f32[128]{0:T(128)S(1)} %log_add_fusion.1, s32[128]{0:T(128)S(1)} %iota_subtract_fusion.1, ...), kind=kOutput, calls=%fused_computation.22 | convolution fusion | flops 2157051904 | bytes 21578756 | tf_op jit(solution)/shard_map/dot_general | solution.py:135
  248.7 3.7 all-to-all-start.1
  252.4 0.8 dynamic_slice.11
  253.2 0.8 gather_fusion
  254.0 6.7 %all-to-all-done.1 = f32[2,64,1024]{2,1,0:T(8,128)S(1)} async-done(((f32[2,64,1024]{2,1,0:T(8,128)}), f32[2,64,1024]{2,1,0:T(8,128)S(1)}, u32[]{:S(2)}, u32[]{:S(2)}) %all-to-all-start.1) | async-done | bytes 524320 | tf_op jit(solution)/shard_map/all_to_all | solution.py:87
  260.7 0.7 stack.2
  261.4 8.9 %all-to-all-start.2 = ((f32[128,1,128]{2,1,0:T(1,128)}), f32[128,1,128]{2,1,0:T(1,128)S(1)}, u32[]{:S(2)}, u32[]{:S(2)}) async-start(f32[128,1,128]{2,1,0:T(1,128)} %stack.2), calls=%async_computation.2 | async-start | bytes 131072 | tf_op jit(solution)/shard_map/all_to_all | solution.py:139
  270.2 0.7 subtract_reduce_fusion
  270.9 6.8 %psum.35 = f32[]{:T(128)} all-reduce(f32[]{:T(128)} %get-tuple-element.7), channel_id=1, replica_groups=mesh['batch_0'=2,'batch_1'=4,'batch_2'=8,'batch_3'=2,'rep'=2] {'batch_0'}, use_global_device_ids=true, to_apply=%region_5.6 | all-reduce | flops 1 | bytes 8 | tf_op jit(solution)/shard_map/psum | solution.py:76
  277.7 10.5 %psum.36 = f32[]{:T(128)} all-reduce(f32[]{:T(128)} %psum.35), channel_id=1, replica_groups=mesh['batch_0'=2,'batch_1'=4,'batch_2'=8,'batch_3'=2,'rep'=2] {'batch_1'}, use_global_device_ids=true, to_apply=%region_6.7 | all-reduce | flops 1 | bytes 8 | tf_op jit(solution)/shard_map/psum | solution.py:76
  288.2 15.4 %psum.37 = f32[]{:T(128)} all-reduce(f32[]{:T(128)} %psum.36), channel_id=1, replica_groups=mesh['batch_0'=2,'batch_1'=4,'batch_2'=8,'batch_3'=2,'rep'=2] {'batch_2'}, use_global_device_ids=true, to_apply=%region_7.8 | all-reduce | flops 1 | bytes 8 | tf_op jit(solution)/shard_map/psum | solution.py:76
  303.6 7.0 %psum.38 = f32[]{:T(128)} all-reduce(f32[]{:T(128)} %psum.37), channel_id=1, replica_groups=mesh['batch_0'=2,'batch_1'=4,'batch_2'=8,'batch_3'=2,'rep'=2] {'batch_3'}, use_global_device_ids=true, to_apply=%region_8.9 | all-reduce | flops 1 | bytes 8 | tf_op jit(solution)/shard_map/psum | solution.py:76
  310.6 5.0 %psum.39 = f32[]{:T(128)} all-reduce(f32[]{:T(128)} %psum.38), channel_id=1, replica_groups=mesh['batch_0'=2,'batch_1'=4,'batch_2'=8,'batch_3'=2,'rep'=2] {'rep'}, use_global_device_ids=true, to_apply=%region_9.10 | all-reduce | flops 1 | bytes 8 | tf_op jit(solution)/shard_map/psum | solution.py:76
  316.3 0.7 reduce_sum.39
  317.0 0.0 all-to-all-done.2
  317.0 63.3 %all-gather.13.cloned.1.call-done = bf16[16384,1024]{1,0:T(8,128)(2,1)} async-done(((bf16[128,1024]{1,0:T(8,128)(2,1)}), bf16[16384,1024]{1,0:T(8,128)(2,1)}) %all-gather.13.cloned.1.call-update) | async-done | bytes 33554448 | tf_op jit(solution)/shard_map/all_gather | solution.py:145
  380.4 0.0 copy-done
  380.4 31.9 %fusion.15 = f32[64,1024]{1,0:T(8,128)} fusion(bf16[16384,1024]{1,0:T(8,128)(2,1)} %all-gather.13.cloned.1.call-done, bf16[64,1024]{1,0:T(8,128)(2,1)S(1)} %copy-done, s32[64]{0:T(128)S(1)} %iota_add_fusion, f32[16384]{0:T(1024)S(1)} %bitcast.308, f32[64]{0:T(128)S(1)} %get-tuple-element.8, f32[]{:T(128)} %bitcast.307, f32[]{:T(128)S(6)} %mul.362), kind=kOutput, calls=%fused_computation.23 | convolution fusion | flops 4303421440 | bytes 34013704 | tf_op jit(solution)/shard_map/dot_general | solution.py:157
  (8 shorter events, 0.1 us)
Async XLA Ops:
  7.2 159.9 %all-gather.11.cloned.1.call-start = ((), (), s32[]{:S(2)}) async-start(), calls=%async_computation.3 | async-start | bytes 16908288 | tf_op jit(solution)/shard_map/all_gather | solution.py:106
  7.9 372.5 %all-gather.13.cloned.1.call-start = ((), (), s32[]{:S(2)}) async-start(), calls=%async_computation.4 | async-start | bytes 33816576 | tf_op jit(solution)/shard_map/all_gather | solution.py:145
  184.8 52.1 %all-to-all-start = ((f32[2,2,128]{2,1,0:T(2,128)}), f32[2,2,128]{2,1,0:T(2,128)S(1)}, u32[]{:S(2)}, u32[]{:S(2)}) async-start(f32[2,2,128]{2,1,0:T(2,128)} %broadcast_in_dim.4), calls=%async_computation | async-start | bytes 4096 | tf_op jit(solution)/shard_map/all_to_all | solution.py:14
  236.9 143.4 %copy-start = (bf16[64,1024]{1,0:T(8,128)(2,1)S(1)}, bf16[64,1024]{1,0:T(8,128)(2,1)}, u32[]{:S(2)}) copy-start(bf16[64,1024]{1,0:T(8,128)(2,1)} %param.4) | copy-start | bytes 393220
  248.7 12.0 %all-to-all-start.1 = ((f32[2,64,1024]{2,1,0:T(8,128)}), f32[2,64,1024]{2,1,0:T(8,128)S(1)}, u32[]{:S(2)}, u32[]{:S(2)}) async-start(f32[2,64,1024]{2,1,0:T(8,128)} %bitcast.46), calls=%async_computation.1 | async-start | bytes 1048576 | tf_op jit(solution)/shard_map/all_to_all | solution.py:87
  261.4 55.6 %all-to-all-start.2 = ((f32[128,1,128]{2,1,0:T(1,128)}), f32[128,1,128]{2,1,0:T(1,128)S(1)}, u32[]{:S(2)}, u32[]{:S(2)}) async-start(f32[128,1,128]{2,1,0:T(1,128)} %stack.2), calls=%async_computation.2 | async-start | bytes 131072 | tf_op jit(solution)/shard_map/all_to_all | solution.py:139
Sparse Core Ops, SparseCore 0:
  11.6 155.4 all-gather.10
  170.7 209.5 all-gather.12
